TPU v7x, 32 devices: a whole 2x2x4 slice. The times are simulated.
32 devices in a mesh: frame: 8 (over z, x), row: 4 (over y, core).
Axes of the slice: x: 2, y: 2, z: 4, core: 2. Of those that a mesh axis runs over, the one named last changes fastest.
Arguments:
- clip: bfloat16 [16, 16, 256, 128], P('frame', 'row'), may hold values from -6 to 6
- first_kernel: bfloat16 [3, 3, 3, 128, 128], replicated, may hold values from -0.109375 to 0.109375
- second_kernel: bfloat16 [3, 3, 3, 128, 128], replicated, may hold values from -0.109375 to 0.109375
- cotangent: bfloat16 [16, 16, 256, 128], P('frame', 'row'), may hold values from -6 to 6
Outputs:
- critic_map: bfloat16 [16, 16, 256, 128], P('frame', 'row')
- clip_grad: bfloat16 [16, 16, 256, 128], P('frame', 'row')
- first_grad: float32 [3, 3, 3, 128, 128], replicated
- second_grad: float32 [3, 3, 3, 128, 128], replicated
All inputs are finite; a program needn't handle non-finite values.
Results may differ from a plain program's by a relative error of at most 0.012.
Values may be sent and summed in bfloat16 or wider, within the bound.
A program may use at most 64 MiB of HBM per device.

v0:
```python
import functools

import jax
import jax.numpy as jnp
from jax import lax
from jax.experimental import pallas as pl
from jax.experimental.pallas import tpu as pltpu
from jax.sharding import PartitionSpec as P

MESH = pl.DeviceIdType.MESH
BF16, F32 = jnp.bfloat16, jnp.float32


def silu_slope(value):
    sigma = jax.nn.sigmoid(value)
    return sigma * (1.0 + value * (1.0 - sigma))


def kernel(
    n_frame, n_row, grad_scale,
    clip, w1, w2, cot,
    critic, clip_grad, g1, g2,
    pads, cols0, cols1, cols2, cols3, w1t, w2t, acc, slope1,
    f_send, f_recv, r_send, r_recv,
):
    cols = (cols0, cols1, cols2, cols3)
    _, rows, width, ch = clip.shape
    me_f, me_r = lax.axis_index("frame"), lax.axis_index("row")
    later, earlier = me_f < n_frame - 1, me_f > 0
    below, above = me_r < n_row - 1, me_r > 0
    sides = (
        (later, {"frame": me_f + 1}), (earlier, {"frame": me_f - 1}),
        (below, {"row": me_r + 1}), (above, {"row": me_r - 1}),
    )
    barrier = pltpu.get_barrier_semaphore()
    for there, who in sides:
        @pl.when(there)
        def _():
            pl.semaphore_signal(barrier, inc=1, device_id=who, device_id_type=MESH)

    def zero(ref):
        ref[...] = jnp.zeros(ref.shape, ref.dtype)

    for k in range(4):
        fwd = k < 2

        @pl.when(jnp.logical_not(earlier if fwd else later))
        def _():
            for f in ((0, 1) if fwd else (2, 3)):
                zero(pads.at[k, f])
        local = (2, 3) if fwd else (0, 1)
        halo = (0, 1) if fwd else (2, 3)
        for f in range(4):
            @pl.when(jnp.logical_not(above))
            def _():
                zero(pads.at[k, f, 0])

            @pl.when(jnp.logical_not(below))
            def _():
                zero(pads.at[k, f, rows + 1])
    for t in range(2):
        pads[0, 2 + t, 1 : rows + 1] = clip[t]
    peers = sum(there.astype(jnp.int32) for there, _ in sides)
    pl.semaphore_wait(barrier, peers)

    def frame_copy(k, t):
        fwd = k < 2
        base, hbase = (2, 0) if fwd else (0, 2)
        return pltpu.make_async_remote_copy(
            src_ref=pads.at[k, base + t, pl.ds(1, rows)],
            dst_ref=pads.at[k, hbase + t, pl.ds(1, rows)],
            send_sem=f_send.at[k, t],
            recv_sem=f_recv.at[k, t],
            device_id={"frame": me_f + 1 if fwd else me_f - 1},
            device_id_type=MESH,
        )

    def row_copy(k, f, way):
        src, dst = ((rows, 0), (1, rows + 1))[way]
        return pltpu.make_async_remote_copy(
            src_ref=pads.at[k, f, src],
            dst_ref=pads.at[k, f, dst],
            send_sem=r_send.at[k, f, way],
            recv_sem=r_recv.at[k, f, way],
            device_id={"row": me_r + 1 if way == 0 else me_r - 1},
            device_id_type=MESH,
        )

    def send_rows(k, f):
        @pl.when(below)
        def _():
            row_copy(k, f, 0).start()

        @pl.when(above)
        def _():
            row_copy(k, f, 1).start()

    def wait_rows(k, f):
        @pl.when(above)
        def _():
            row_copy(k, f, 0).wait_recv()

        @pl.when(below)
        def _():
            row_copy(k, f, 1).wait_recv()

    def publish(k, t):
        @pl.when(later if k < 2 else earlier)
        def _():
            frame_copy(k, t).start()
        send_rows(k, (2 if k < 2 else 0) + t)

    def build(k, f):
        def one(r, c):
            x = pads[k, f, r].astype(F32)
            pos = lax.broadcasted_iota(jnp.int32, (width, ch), 0)
            left = jnp.where(pos == 0, 0.0, pltpu.roll(x, 1, 0))
            right = jnp.where(pos == width - 1, 0.0, pltpu.roll(x, width - 1, 0))
            cols[k][f, r, :, 0:ch] = left.astype(BF16)
            cols[k][f, r, :, ch : 2 * ch] = pads[k, f, r]
            cols[k][f, r, :, 2 * ch : 3 * ch] = right.astype(BF16)
            return c
        lax.fori_loop(0, rows + 2, one, 0)

    STEP = 2

    def taps(k, w, t, frames, h, z):
        for a in range(3):
            if t + a not in frames:
                continue
            for b in range(3):
                x = cols[k][t + a, pl.ds(h * STEP + b, STEP)].reshape(STEP * width, 3 * ch)
                d = jnp.dot(x, w[a, b], preferred_element_type=F32)
                z = d if z is None else z + d
        return z

    def stage(k, w, epilogue, between):
        fwd = k < 2
        order = (1, 0) if fwd else (0, 1)
        local, halo = ((2, 3), (0, 1)) if fwd else ((0, 1), (2, 3))
        for t in order:
            wait_rows(k, local[t])
            build(k, local[t])
        for t in order:
            def part(h, c):
                z = taps(k, w, t, local, h, None)
                acc[t, pl.ds(h * STEP, STEP)] = z.reshape(STEP, width, ch)
                return c
            lax.fori_loop(0, rows // STEP, part, 0)
        between()
        for t in order:
            @pl.when(earlier if fwd else later)
            def _():
                frame_copy(k, t).wait_recv()
                send_rows(k, halo[t])
                wait_rows(k, halo[t])
            build(k, halo[t])

            def rest(h, c):
                z = taps(k, w, t, halo, h, acc[t, pl.ds(h * STEP, STEP)].reshape(STEP * width, ch))
                epilogue(t, pl.ds(h * STEP, STEP), h * STEP, z.reshape(STEP, width, ch))
                return c
            lax.fori_loop(0, rows // STEP, rest, 0)
            if k < 3:
                publish(k + 1, t)

    for t in (1, 0):
        publish(0, t)

    def turn_weights():
        def one(i, c):
            a, b = i // 3, lax.rem(i, 3)
            for src, dst in ((w1, w1t), (w2, w2t)):
                for q in range(3):
                    block = src[2 - a, 2 - b, pl.ds((2 - q) * ch, ch), :]
                    dst[a, b, pl.ds(q * ch, ch), :] = block.astype(F32).T.astype(BF16)
            return c
        lax.fori_loop(0, 9, one, 0)

    def weight_grad(kx, kd, out):
        def one(i, c):
            a, b = i // 3, lax.rem(i, 3)
            total = None
            for t in range(2):
                x = cols[kx][t + a, pl.ds(b, rows)].reshape(rows * width, 3 * ch)
                d = pads[kd, t, 1 : rows + 1].reshape(rows * width, ch)
                p = lax.dot_general(x, d, (((0,), (0,)), ((), ())), preferred_element_type=F32)
                total = p if total is None else total + p
            out[a, b] = (total * grad_scale).astype(out.dtype)
            return c
        lax.fori_loop(0, 9, one, 0)

    def end0(t, hs, h, z):
        sigma = jax.nn.sigmoid(z)
        slope1[t, hs] = sigma * (1.0 + z * (1.0 - sigma))
        pads[1, 2 + t, pl.ds(h + 1, STEP)] = (z * sigma).astype(BF16)

    def end1(t, hs, h, z):
        sigma = jax.nn.sigmoid(z)
        critic[t, hs] = (z * sigma).astype(BF16)
        delta = cot[t, hs].astype(F32) * (sigma * (1.0 + z * (1.0 - sigma)))
        pads[2, t, pl.ds(h + 1, STEP)] = delta.astype(BF16)

    def end2(t, hs, h, z):
        pads[3, t, pl.ds(h + 1, STEP)] = (z * slope1[t, hs]).astype(BF16)

    def end3(t, hs, h, z):
        clip_grad[t, hs] = z.astype(BF16)

    stage(0, w1, end0, turn_weights)
    stage(1, w2, end1, lambda: None)
    stage(2, w2t, end2, lambda: weight_grad(1, 2, g2))
    stage(3, w1t, end3, lambda: weight_grad(0, 3, g1))

    for k in range(4):
        fwd = k < 2
        for t in range(2):
            @pl.when(later if fwd else earlier)
            def _():
                frame_copy(k, t).wait_send()
        for f in range(4):
            is_halo = (f < 2) if fwd else (f >= 2)
            has = (earlier if fwd else later) if is_halo else jnp.bool_(True)
            for way, there in ((0, below), (1, above)):
                @pl.when(jnp.logical_and(there, has) if is_halo else there)
                def _():
                    row_copy(k, f, way).wait_send()


def on_device(n_frame, n_row, clip, first_kernel, second_kernel, cotangent):
    frames, rows, width, ch = clip.shape
    grad_scale = 1.0 / float(frames * n_frame * rows * n_row * width) ** 0.5
    vmem = pl.BlockSpec(memory_space=pltpu.VMEM)
    cols = pltpu.VMEM((4, rows + 2, width, 3 * ch), BF16)
    weights = (3, 3, 3 * ch, ch)
    critic, clip_grad, g1, g2 = pl.pallas_call(
        functools.partial(kernel, n_frame, n_row, grad_scale),
        out_shape=(
            jax.ShapeDtypeStruct(clip.shape, BF16),
            jax.ShapeDtypeStruct(clip.shape, BF16),
            jax.ShapeDtypeStruct(weights, BF16),
            jax.ShapeDtypeStruct(weights, BF16),
        ),
        in_specs=[vmem] * 4,
        out_specs=(vmem,) * 4,
        scratch_shapes=[
            pltpu.VMEM((4, 4, rows + 2, width, ch), BF16),
            cols, cols, cols, cols,
            pltpu.VMEM(weights, BF16),
            pltpu.VMEM(weights, BF16),
            pltpu.VMEM(clip.shape, F32),
            pltpu.VMEM(clip.shape, F32),
            pltpu.SemaphoreType.DMA((4, 2)),
            pltpu.SemaphoreType.DMA((4, 2)),
            pltpu.SemaphoreType.DMA((4, 4, 2)),
            pltpu.SemaphoreType.DMA((4, 4, 2)),
        ],
        compiler_params=pltpu.CompilerParams(
            collective_id=0, has_side_effects=True, vmem_limit_bytes=60 * 2**20
        ),
    )(clip, first_kernel.reshape(weights), second_kernel.reshape(weights), cotangent)
    g1, g2 = lax.psum((g1, g2), ("frame", "row"))
    shape = first_kernel.shape
    return critic, clip_grad, g1.astype(F32).reshape(shape), g2.astype(F32).reshape(shape)


def solution(mesh):
    placed = (P("frame", "row", None, None), P(), P(), P("frame", "row", None, None))
    return jax.shard_map(
        functools.partial(on_device, mesh.shape["frame"], mesh.shape["row"]),
        mesh=mesh,
        in_specs=placed,
        out_specs=(P("frame", "row", None, None), P("frame", "row", None, None), P(), P()),
        check_vma=False,
    )
```

profile of v0, /device:TPU:0, one launch (start us, length us, event | category | flops | bytes accessed | tf_op | source)
XLA Modules:
  0.0 235.2 jit_solution(17794383163298847573)
XLA Ops:
  7.2 0.0 all-reduce.3.cloned.1.call-start
  7.2 74.2 %shard_map.75 = (bf16[2,4,256,128]{3,2,1,0:T(8,128)(2,1)}, bf16[2,4,256,128]{3,2,1,0:T(8,128)(2,1)}, bf16[3,3,384,128]{3,2,1,0:T(8,128)(2,1)}, bf16[3,3,384,128]{3,2,1,0:T(8,128)(2,1)}) custom-call(bf16[2,4,256,128]{3,2,1,0:T(8,128)(2,1)} %clip.1, bf16[3,3,384,128]{3,2,1,0:T(8,128)(2,1)} %bitcast.4, bf16[3,3,384,128]{3,2,1,0:T(8,128)(2,1)} %bitcast.5, ...), custom_call_target="tpu_custom_call" | custom-call | tf_op jit(solution)/shard_map/pallas_call | solution.py:236
  81.4 0.0 all-reduce.3.cloned.1.call-update
  81.5 141.3 %all-reduce.3.cloned.1.call-done = (bf16[3,3,3,128,128]{4,3,2,1,0:T(8,128)(2,1)}, bf16[3,3,3,128,128]{4,3,2,1,0:T(8,128)(2,1)}) async-done(((bf16[3,3,3,128,128]{4,3,2,1,0:T(8,128)(2,1)}, bf16[3,3,3,128,128]{4,3,2,1,0:T(8,128)(2,1)}), (bf16[3,3,3,128,128]{4,3,2,1,0:T(8,128)(2,1)}, bf16[3,3,3,128,128]{4,3,2,1,0:T(8,128)(2,1)})) %all-reduce.3.cloned.1.call-update) | async-done | bytes 1769488 | tf_op jit(solution)/shard_map/psum | solution.py:262
  222.7 0.0 copy-start
  222.7 2.7 %reshape.29 = f32[3,3,3,128,128]{4,3,2,1,0:T(8,128)} convert(bf16[3,3,3,128,128]{4,3,2,1,0:T(8,128)(2,1)} %get-tuple-element.12) | non-fusion elementwise | flops 442368 | bytes 2654208 | tf_op jit(solution)/shard_map/reshape | solution.py:264
  225.4 0.0 copy-start.2
  225.4 0.0 copy-done
  225.4 0.0 copy-start.1
  225.4 1.4 reshape.31
  226.8 0.0 copy-done.2
  226.8 0.8 copy.12
  227.6 0.0 copy-done.1
  227.6 0.8 copy.13
Async XLA Ops:
  7.2 215.6 %all-reduce.3.cloned.1.call-start = ((), (), s32[]{:S(2)}) async-start(), calls=%async_computation | async-start | bytes 3538944 | tf_op jit(solution)/shard_map/psum | solution.py:262
  222.7 2.7 %copy-start = (bf16[3,3,3,128,128]{4,3,2,1,0:T(8,128)(2,1)S(1)}, bf16[3,3,3,128,128]{4,3,2,1,0:T(8,128)(2,1)}, u32[]{:S(2)}) copy-start(bf16[3,3,3,128,128]{4,3,2,1,0:T(8,128)(2,1)} %get-tuple-element.13) | copy-start | bytes 2654212
  225.4 1.4 copy-start.2
  225.4 2.2 copy-start.1
Sparse Core Ops, SparseCore 0:
  81.6 141.0 all-reduce.2
where the time goes:
time: 235 us
  waiting for transfers between devices  141 us (60%)
  Pallas kernels  74.2 us (32%)
  between operations  14 us (6%)
  other arithmetic  4.07 us (2%)
    psum x1, waiting for transfers between devices, on_device(): g1, g2 = lax.psum((g1, g2), ('frame', 'row'))  141 us
    pallas_call x1, Pallas kernels, on_device(): pl.pallas_call(functools.partial(kernel, n_frame, n_row, grad_scale), out...  74.2 us
  transfers between devices with their start and end apart: 1, of which 1 were waited for; matrix products, arithmetic and copies ran while one was open for 0% of the time, Pallas kernels for 0%

commit v1 on v0

--- a/solution.py
+++ b/solution.py
@@ -225,6 +225,73 @@
                 @pl.when(jnp.logical_and(there, has) if is_halo else there)
                 def _():
                     row_copy(k, f, way).wait_send()
+
+
+def sum_kernel(levels, n, mine, total, buf, landing, s1, q1, s2, q2):
+    peers = []
+    for axis, step in levels:
+        me = lax.axis_index(axis)
+        bit = lax.rem(me // step, 2)
+        peers.append((bit, {axis: me + (1 - 2 * bit) * step}))
+    barrier = pltpu.get_barrier_semaphore()
+    for _, who in peers:
+        pl.semaphore_signal(barrier, inc=1, device_id=who, device_id_type=MESH)
+    pl.semaphore_wait(barrier, len(peers))
+    lo, size = 0, n
+    for j, (bit, who) in enumerate(peers):
+        size //= 2
+        keep, give = lo + bit * size, lo + (1 - bit) * size
+        src = mine if j == 0 else buf
+        copy = pltpu.make_async_remote_copy(
+            src_ref=src.at[pl.ds(give, size)],
+            dst_ref=landing.at[pl.ds(size, size)],
+            send_sem=s1.at[j], recv_sem=q1.at[j],
+            device_id=who, device_id_type=MESH,
+        )
+        copy.start()
+        copy.wait()
+        last = size == 1
+
+        def add(i, c):
+            z = src[keep + i].astype(F32) + landing[size + i].astype(F32)
+            dst = total if last else buf
+            dst[keep + i] = z.astype(BF16)
+            return c
+        lax.fori_loop(0, size, add, 0)
+        lo = keep
+    for j in range(len(peers) - 1, -1, -1):
+        bit, who = peers[j]
+        copy = pltpu.make_async_remote_copy(
+            src_ref=total.at[pl.ds(lo, size)],
+            dst_ref=total.at[pl.ds(lo, size)],
+            send_sem=s2.at[j], recv_sem=q2.at[j],
+            device_id=who, device_id_type=MESH,
+        )
+        copy.start()
+        copy.wait()
+        lo, size = lo - bit * size, size * 2
+
+
+def summed(n_frame, n_row, flat):
+    n = n_frame * n_row
+    levels = [("row", 1 << b) for b in range(n_row.bit_length() - 1)]
+    levels += [("frame", 1 << b) for b in range(n_frame.bit_length() - 1)]
+    length, ch = flat.shape
+    chunk = -(-length // (16 * n)) * 16
+    mine = jnp.pad(flat, ((0, chunk * n - length), (0, 0))).reshape(n, chunk, ch)
+    vmem = pl.BlockSpec(memory_space=pltpu.VMEM)
+    sems = pltpu.SemaphoreType.DMA((len(levels),))
+    out = pl.pallas_call(
+        functools.partial(sum_kernel, levels, n),
+        out_shape=jax.ShapeDtypeStruct(mine.shape, BF16),
+        in_specs=[vmem],
+        out_specs=vmem,
+        scratch_shapes=[pltpu.VMEM(mine.shape, BF16), pltpu.VMEM(mine.shape, BF16), sems, sems, sems, sems],
+        compiler_params=pltpu.CompilerParams(
+            collective_id=1, has_side_effects=True, vmem_limit_bytes=32 * 2**20
+        ),
+    )(mine)
+    return out.reshape(n * chunk, ch)[:length]
 
 
 def on_device(n_frame, n_row, clip, first_kernel, second_kernel, cotangent):
@@ -259,8 +326,10 @@
             collective_id=0, has_side_effects=True, vmem_limit_bytes=60 * 2**20
         ),
     )(clip, first_kernel.reshape(weights), second_kernel.reshape(weights), cotangent)
-    g1, g2 = lax.psum((g1, g2), ("frame", "row"))
     shape = first_kernel.shape
+    flat = jnp.concatenate([g1.reshape(-1, ch), g2.reshape(-1, ch)])
+    both = summed(n_frame, n_row, flat)
+    g1, g2 = both[: both.shape[0] // 2], both[both.shape[0] // 2 :]
     return critic, clip_grad, g1.astype(F32).reshape(shape), g2.astype(F32).reshape(shape)
 
 

time: 235 us -> 143 us (0.61)
  waiting for transfers between devices: 141 us -> 0 us
  Pallas kernels: 74.2 us -> 136 us
  between operations: 14 us -> 0.66 us
    psum x1 -> x0, waiting for transfers between devices: 141 us -> none  [on_device(): g1, g2 = lax.psum((g1, g2), ('frame', 'row'))]
    pallas_call x0 -> x1, Pallas kernels: none -> 61.7 us  [summed(): pl.pallas_call(functools.partial(sum_kernel, levels, n), out_shape=jax.Sh...]
  transfers between devices with their start and end apart: 1 -> 0, of which waited for: 1 -> 0; matrix products, arithmetic and copies ran while one was open for 0% -> 0% of each run, Pallas kernels for 0% -> 0%
where the time goes in v1:
time: 143 us
  Pallas kernels  136 us (95%)
  other arithmetic  4.37 us (3%)
  local copies, waits for them, and re-layouts  1.71 us (1%)
    pallas_call x1, Pallas kernels, on_device(): pl.pallas_call(functools.partial(kernel, n_frame, n_row, grad_scale), out...  74.2 us
    pallas_call x1, Pallas kernels, summed(): pl.pallas_call(functools.partial(sum_kernel, levels, n), out_shape=jax.Sh...  61.7 us

profile of v1, /device:TPU:0, one launch (start us, length us, event | category | flops | bytes accessed | tf_op | source)
XLA Modules:
  0.0 142.7 jit_solution(9380060440367546247)
XLA Ops:
  0.6 74.2 %shard_map.75 = (bf16[2,4,256,128]{3,2,1,0:T(8,128)(2,1)}, bf16[2,4,256,128]{3,2,1,0:T(8,128)(2,1)}, bf16[3,3,384,128]{3,2,1,0:T(8,128)(2,1)}, bf16[3,3,384,128]{3,2,1,0:T(8,128)(2,1)}) custom-call(bf16[2,4,256,128]{3,2,1,0:T(8,128)(2,1)} %clip.1, bf16[3,3,384,128]{3,2,1,0:T(8,128)(2,1)} %bitcast.16, bf16[3,3,384,128]{3,2,1,0:T(8,128)(2,1)} %bitcast.17, ...), custom_call_target="tpu_custom_call" | custom-call | tf_op jit(solution)/shard_map/pallas_call | solution.py:303
  74.9 1.6 %fusion.2 = bf16[7168,128]{1,0:T(8,128)(2,1)S(1)} fusion(bf16[3456,128]{1,0:T(8,128)(2,1)} %bitcast.15, bf16[3456,128]{1,0:T(8,128)(2,1)} %bitcast.14), kind=kLoop, calls=%fused_computation.3 | loop fusion | flops 6422528 | bytes 3604480 | tf_op jit(solution)/shard_map/concatenate | solution.py:330
  76.4 61.7 %shard_map.76 = bf16[32,224,128]{2,1,0:T(8,128)(2,1)S(1)} custom-call(bf16[32,224,128]{2,1,0:T(8,128)(2,1)S(1)} %bitcast.10), custom_call_target="tpu_custom_call" | custom-call | tf_op jit(solution)/shard_map/pallas_call | solution.py:284
  138.2 0.1 fusion.3
  138.3 1.4 convert.2
  139.7 0.0 copy-start.1
  139.7 0.0 copy-start
  139.7 1.4 convert.3
  141.1 0.0 copy-done.1
  141.1 0.8 copy.10
  141.9 0.0 copy-done
  141.9 0.8 copy.11
Async XLA Ops:
  139.7 1.4 copy-start.1
  139.7 2.2 %copy-start = (bf16[2,4,256,128]{3,2,1,0:T(8,128)(2,1)S(1)}, bf16[2,4,256,128]{3,2,1,0:T(8,128)(2,1)}, u32[]{:S(2)}) copy-start(bf16[2,4,256,128]{3,2,1,0:T(8,128)(2,1)} %get-tuple-element.19) | copy-start | bytes 1572868
